TPU v7x, 1024 devices: a whole 4x4x32 slice. The times are simulated.
1024 devices in a mesh: gx: 16 (over z_hi, x, core), gy: 4 (over y), gz: 16 (over z_lo).
Axes of the slice: x: 4, y: 4, z: 32 (z_hi: 2, z_lo: 16; z = z_hi * 16 + z_lo), core: 2. Of those that a mesh axis runs over, the one named last changes fastest.
Arguments:
- solution: float32 [16, 32, 64, 512], P(None, 'gx', 'gz', 'gy'), may hold values from -0.6 to 0.6
- residual: float32 [16, 32, 64, 512], P(None, 'gx', 'gz', 'gy'), may hold values from -6 to 6
- direction_prev: float32 [16, 32, 64, 512], P(None, 'gx', 'gz', 'gy'), may hold values from -0.3 to 0.3, as said below
- image_prev: float32 [16, 32, 64, 512], P(None, 'gx', 'gz', 'gy'), may hold values from -9 to 9, as said below
- gram_prev: float32 [16, 16], replicated, may hold values from -1048576 to 1048576, as said below
Outputs:
- solution_new: float32 [16, 32, 64, 512], P(None, 'gx', 'gz', 'gy')
- residual_new: float32 [16, 32, 64, 512], P(None, 'gx', 'gz', 'gy')
- direction: float32 [16, 32, 64, 512], P(None, 'gx', 'gz', 'gy')
Inputs may be any that keep to these rules, and one draw needn't show every extreme that they name: direction_prev is a field of order 0.05. image_prev equals A direction_prev, computed in float32. gram_prev is symmetric and positive definite.
All inputs are finite; a program needn't handle non-finite values.
Results may differ from a plain program's by a relative error of at most 0.0001.
Values sent between devices are 32-bit elements; how exact they have to be, the bound alone decides.
A program may use at most 64 MiB of HBM per device.

v0:
```python
import jax
import jax.numpy as jnp
from jax import lax
from jax.sharding import Mesh
from jax.sharding import PartitionSpec as P

GX_GY_GZ = ("gx_0", "gx_1", "gx_2", "gy", "gz")
GX = ("gx_0", "gx_1", "gx_2")


def with_halo(value, sides, width):
    for axis, dim in sides:
        devices, length = (lax.axis_size(axis), value.shape[dim])
        up = [(i, (i + 1) % devices) for i in range(devices - 1)]
        down = [(j, i) for i, j in up]
        last = lax.slice_in_dim(value, length - width, length, axis=dim)
        first = lax.slice_in_dim(value, 0, width, axis=dim)
        before = lax.ppermute(last, axis, up)
        after = lax.ppermute(first, axis, down)
        value = jnp.concatenate([before, value, after], axis=dim)
    return value


def one_axis_at_a_time(value, axes):
    for axis in axes:
        value = lax.psum(value, axis)
    return value


def box_sum(padded):
    total = padded[:, :-2] + padded[:, 1:-1] + padded[:, 2:]
    total = total[:, :, :-2] + total[:, :, 1:-1] + total[:, :, 2:]
    return total[:, :, :, :-2] + total[:, :, :, 1:-1] + total[:, :, :, 2:]


def colors_of(shape):
    first = lax.broadcasted_iota(jnp.int32, shape, 1) % 2
    second = lax.broadcasted_iota(jnp.int32, shape, 2) % 2
    third = lax.broadcasted_iota(jnp.int32, shape, 3) % 2
    return 4 * first + 2 * second + third


def local_gram(left, right):
    return jnp.einsum("kxzy,lxzy->kl", left, right, precision=lax.Precision.HIGHEST)


def combine(field, mixing):
    return jnp.einsum("kxzy,kl->lxzy", field, mixing, precision=lax.Precision.HIGHEST)


def spd_solve(matrix, target):
    order = matrix.shape[0]
    sym = 0.5 * (matrix + matrix.T)
    lower = jnp.zeros_like(sym)
    for col in range(order):
        column = sym[col:, col] - jnp.sum(lower[col:, :col] * lower[col, :col][None, :], axis=1)
        pivot = jnp.sqrt(column[0])
        lower = lower.at[col:, col].set(column / pivot)
    middle = jnp.zeros_like(target)
    for row in range(order):
        value = target[row] - jnp.sum(lower[row, :row][:, None] * middle[:row], axis=0)
        middle = middle.at[row].set(value / lower[row, row])
    answer = jnp.zeros_like(target)
    for row in range(order - 1, -1, -1):
        value = middle[row] - jnp.sum(lower[row + 1 :, row][:, None] * answer[row + 1 :], axis=0)
        answer = answer.at[row].set(value / lower[row, row])
    return answer


def sweep_box(field):
    padded = with_halo(field, ((GX, 1), ("gy", 3), ("gz", 2)), 1)
    return box_sum(padded)


def body(solution, residual, direction_prev, image_prev, gram_prev):
    colors = colors_of(residual.shape)
    smoothed = jnp.where(colors == 0, residual / 26.0, jnp.float32(0.0))
    for shade in list(range(1, 8)) + list(range(6, -1, -1)):
        boxed = sweep_box(smoothed)
        smoothed = jnp.where(colors == shade, (residual + boxed - smoothed) / 26.0, smoothed)
    padded = with_halo(smoothed, ((GX, 1), ("gy", 3), ("gz", 2)), 1)
    image = 27.0 * smoothed - box_sum(padded)
    gram_zr = one_axis_at_a_time(local_gram(smoothed, residual), GX_GY_GZ)
    beta_mix = spd_solve(gram_prev, gram_zr)
    direction = smoothed + combine(direction_prev, beta_mix)
    image_new = image + combine(image_prev, beta_mix)
    curvature = one_axis_at_a_time(local_gram(direction, image_new), GX_GY_GZ)
    alpha_step = spd_solve(curvature, gram_zr)
    solution_new = solution + combine(direction, alpha_step)
    residual_new = residual - combine(image_new, alpha_step)
    return (solution_new, residual_new, direction)


def solution(mesh):
    split = Mesh(
        mesh.devices.reshape(2, 4, 2, mesh.shape["gy"], mesh.shape["gz"]),
        ("gx_0", "gx_1", "gx_2", "gy", "gz"),
    )
    in_specs = (
        P(None, GX, "gz", "gy"),
        P(None, GX, "gz", "gy"),
        P(None, GX, "gz", "gy"),
        P(None, GX, "gz", "gy"),
        P(),
    )
    out_specs = (P(None, GX, "gz", "gy"), P(None, GX, "gz", "gy"), P(None, GX, "gz", "gy"))
    return jax.shard_map(body, mesh=split, in_specs=in_specs, out_specs=out_specs, check_vma=False)
```

profile of v0, /device:TPU:1, one launch (start us, length us, event | category | flops | bytes accessed | tf_op | source)
XLA Modules:
  0.0 1049.2 jit_solution(14665390847853913356)
XLA Ops:
  1.7 4.5 collective-permute-start
  6.2 12.8 %collective-permute-start.1 = (f32[16,1,4,128]{3,0,2,1:T(8,128)S(1)}, f32[16,1,4,128]{3,0,2,1:T(8,128)S(1)}, u32[]{:S(2)}, u32[]{:S(2)}) collective-permute-start(f32[16,1,4,128]{3,0,2,1:T(8,128)S(1)} %get-tuple-element.1258), channel_id=1, source_target_pairs={{64,0},{128,64},{192,128},{256,192},{320,256},{384,320},{448,384},... | collective-permute-start | bytes 98312 | tf_op jit(solution)/shard_map/ppermute | solution.py:19
  37.1 4.2 collective-permute-done.3
  60.2 4.1 collective-permute-done.9
  67.6 4.6 collective-permute-done.11
  72.6 5.0 collective-permute-start.12
  87.8 3.8 collective-permute-done.15
  91.8 4.9 collective-permute-start.16
  98.3 4.2 collective-permute-done.17
  102.8 7.8 collective-permute-start.18
  112.7 18.1 %collective-permute-done.19 = f32[16,1,4,128]{3,0,2,1:T(8,128)S(1)} collective-permute-done((f32[16,1,4,128]{3,0,2,1:T(8,128)S(1)}, f32[16,1,4,128]{3,0,2,1:T(8,128)S(1)}, u32[]{:S(2)}, u32[]{:S(2)}) %collective-permute-start.19) | collective-permute-done | bytes 32800 | tf_op jit(solution)/shard_map/ppermute | solution.py:19
  134.8 3.8 collective-permute-done.21
  138.7 3.7 collective-permute-start.22
  144.0 3.4 collective-permute-done.23
  147.8 22.3 %collective-permute-start.24 = (f32[16,1,4,128]{3,0,2,1:T(8,128)S(1)}, f32[16,1,4,128]{3,0,2,1:T(8,128)S(1)}, u32[]{:S(2)}, u32[]{:S(2)}) collective-permute-start(f32[16,1,4,128]{3,0,2,1:T(8,128)S(1)} %get-tuple-element.1249), channel_id=1, source_target_pairs={{0,64},{64,128},{128,192},{192,256},{256,320},{320,384},{384,448},... | collective-permute-start | bytes 98312 | tf_op jit(solution)/shard_map/ppermute | solution.py:18
  172.0 18.5 %collective-permute-done.25 = f32[16,1,4,128]{3,0,2,1:T(8,128)S(1)} collective-permute-done((f32[16,1,4,128]{3,0,2,1:T(8,128)S(1)}, f32[16,1,4,128]{3,0,2,1:T(8,128)S(1)}, u32[]{:S(2)}, u32[]{:S(2)}) %collective-permute-start.25) | collective-permute-done | bytes 32800 | tf_op jit(solution)/shard_map/ppermute | solution.py:19
  194.4 3.8 collective-permute-done.27
  202.8 3.7 collective-permute-done.29
  206.9 9.5 collective-permute-start.30
  218.3 18.7 %collective-permute-done.31 = f32[16,1,4,128]{3,0,2,1:T(8,128)S(1)} collective-permute-done((f32[16,1,4,128]{3,0,2,1:T(8,128)S(1)}, f32[16,1,4,128]{3,0,2,1:T(8,128)S(1)}, u32[]{:S(2)}, u32[]{:S(2)}) %collective-permute-start.31) | collective-permute-done | bytes 32800 | tf_op jit(solution)/shard_map/ppermute | solution.py:19
  241.0 3.8 collective-permute-done.33
  249.2 3.7 collective-permute-done.35
  253.3 9.4 collective-permute-start.36
  264.6 18.7 %collective-permute-done.37 = f32[16,1,4,128]{3,0,2,1:T(8,128)S(1)} collective-permute-done((f32[16,1,4,128]{3,0,2,1:T(8,128)S(1)}, f32[16,1,4,128]{3,0,2,1:T(8,128)S(1)}, u32[]{:S(2)}, u32[]{:S(2)}) %collective-permute-start.37) | collective-permute-done | bytes 32800 | tf_op jit(solution)/shard_map/ppermute | solution.py:19
  287.3 3.8 collective-permute-done.39
  295.6 3.7 collective-permute-done.41
  299.7 9.2 collective-permute-start.42
  310.9 18.5 %collective-permute-done.43 = f32[16,1,4,128]{3,0,2,1:T(8,128)S(1)} collective-permute-done((f32[16,1,4,128]{3,0,2,1:T(8,128)S(1)}, f32[16,1,4,128]{3,0,2,1:T(8,128)S(1)}, u32[]{:S(2)}, u32[]{:S(2)}) %collective-permute-start.43) | collective-permute-done | bytes 32800 | tf_op jit(solution)/shard_map/ppermute | solution.py:19
  333.7 3.8 collective-permute-done.45
  342.5 3.5 collective-permute-done.47
  346.3 9.5 collective-permute-start.48
  357.8 19.0 %collective-permute-done.49 = f32[16,1,4,128]{3,0,2,1:T(8,128)S(1)} collective-permute-done((f32[16,1,4,128]{3,0,2,1:T(8,128)S(1)}, f32[16,1,4,128]{3,0,2,1:T(8,128)S(1)}, u32[]{:S(2)}, u32[]{:S(2)}) %collective-permute-start.49) | collective-permute-done | bytes 32800 | tf_op jit(solution)/shard_map/ppermute | solution.py:19
  380.8 3.8 collective-permute-done.51
  393.2 9.1 collective-permute-start.54
  404.5 18.4 %collective-permute-done.55 = f32[16,1,4,128]{3,0,2,1:T(8,128)S(1)} collective-permute-done((f32[16,1,4,128]{3,0,2,1:T(8,128)S(1)}, f32[16,1,4,128]{3,0,2,1:T(8,128)S(1)}, u32[]{:S(2)}, u32[]{:S(2)}) %collective-permute-start.55) | collective-permute-done | bytes 32800 | tf_op jit(solution)/shard_map/ppermute | solution.py:19
  427.1 3.8 collective-permute-done.57
  435.7 3.5 collective-permute-done.59
  439.6 9.5 collective-permute-start.60
  451.2 18.9 %collective-permute-done.61 = f32[16,1,4,128]{3,0,2,1:T(8,128)S(1)} collective-permute-done((f32[16,1,4,128]{3,0,2,1:T(8,128)S(1)}, f32[16,1,4,128]{3,0,2,1:T(8,128)S(1)}, u32[]{:S(2)}, u32[]{:S(2)}) %collective-permute-start.61) | collective-permute-done | bytes 32800 | tf_op jit(solution)/shard_map/ppermute | solution.py:19
  474.1 3.8 collective-permute-done.63
  482.3 3.5 collective-permute-done.65
  486.2 9.4 collective-permute-start.66
  497.7 18.8 %collective-permute-done.67 = f32[16,1,4,128]{3,0,2,1:T(8,128)S(1)} collective-permute-done((f32[16,1,4,128]{3,0,2,1:T(8,128)S(1)}, f32[16,1,4,128]{3,0,2,1:T(8,128)S(1)}, u32[]{:S(2)}, u32[]{:S(2)}) %collective-permute-start.67) | collective-permute-done | bytes 32800 | tf_op jit(solution)/shard_map/ppermute | solution.py:19
  520.4 3.8 collective-permute-done.69
  528.7 3.5 collective-permute-done.71
  532.6 9.4 collective-permute-start.72
  544.2 18.7 %collective-permute-done.73 = f32[16,1,4,128]{3,0,2,1:T(8,128)S(1)} collective-permute-done((f32[16,1,4,128]{3,0,2,1:T(8,128)S(1)}, f32[16,1,4,128]{3,0,2,1:T(8,128)S(1)}, u32[]{:S(2)}, u32[]{:S(2)}) %collective-permute-start.73) | collective-permute-done | bytes 32800 | tf_op jit(solution)/shard_map/ppermute | solution.py:19
  566.8 3.8 collective-permute-done.75
  575.0 3.5 collective-permute-done.77
  578.9 9.4 collective-permute-start.78
  590.5 18.7 %collective-permute-done.79 = f32[16,1,4,128]{3,0,2,1:T(8,128)S(1)} collective-permute-done((f32[16,1,4,128]{3,0,2,1:T(8,128)S(1)}, f32[16,1,4,128]{3,0,2,1:T(8,128)S(1)}, u32[]{:S(2)}, u32[]{:S(2)}) %collective-permute-start.79) | collective-permute-done | bytes 32800 | tf_op jit(solution)/shard_map/ppermute | solution.py:19
  613.1 3.8 collective-permute-done.81
  625.4 9.4 collective-permute-start.84
  636.8 67.3 %psum.70 = f32[16,16]{1,0:T(8,128)S(1)} all-reduce(f32[16,16]{1,0:T(8,128)S(1)} %convolution_bitcast_fusion.1), channel_id=1, replica_groups=mesh['gx_0'=2,'gx_1'=4,'gx_2'=2,'gy'=4,'gz'=16] {'gx_0'}, use_global_device_ids=true, to_apply=%region_0.1 | all-reduce | flops 256 | bytes 2048 | tf_op jit(solution)/shard_map/psum | solution.py:26
  704.1 28.2 %psum.71 = f32[16,16]{1,0:T(8,128)S(1)} all-reduce(f32[16,16]{1,0:T(8,128)S(1)} %psum.70), channel_id=1, replica_groups=mesh['gx_0'=2,'gx_1'=4,'gx_2'=2,'gy'=4,'gz'=16] {'gx_1'}, use_global_device_ids=true, to_apply=%region_1.2 | all-reduce | flops 256 | bytes 2048 | tf_op jit(solution)/shard_map/psum | solution.py:26
  732.2 4.9 psum.72
  737.1 6.1 psum.73
  743.2 82.6 %psum.74 = f32[16,16]{1,0:T(8,128)S(1)} all-reduce(f32[16,16]{1,0:T(8,128)S(1)} %psum.73), channel_id=1, replica_groups=mesh['gx_0'=2,'gx_1'=4,'gx_2'=2,'gy'=4,'gz'=16] {'gz'}, use_global_device_ids=true, to_apply=%region_4.5 | all-reduce | flops 256 | bytes 2048 | tf_op jit(solution)/shard_map/psum | solution.py:26
  854.4 3.7 collective-permute-done.87
  866.5 22.6 %psum.75 = f32[16,16]{1,0:T(8,128)S(1)} all-reduce(f32[16,16]{1,0:T(8,128)S(1)} %convolution_bitcast_fusion), channel_id=1, replica_groups=mesh['gx_0'=2,'gx_1'=4,'gx_2'=2,'gy'=4,'gz'=16] {'gx_0'}, use_global_device_ids=true, to_apply=%region_48.49 | all-reduce | flops 256 | bytes 2048 | tf_op jit(solution)/shard_map/psum | solution.py:26
  889.1 8.4 psum.76
  897.5 16.9 %psum.77 = f32[16,16]{1,0:T(8,128)S(1)} all-reduce(f32[16,16]{1,0:T(8,128)S(1)} %psum.76), channel_id=1, replica_groups=mesh['gx_0'=2,'gx_1'=4,'gx_2'=2,'gy'=4,'gz'=16] {'gx_2'}, use_global_device_ids=true, to_apply=%region_50.51 | all-reduce | flops 256 | bytes 2048 | tf_op jit(solution)/shard_map/psum | solution.py:26
  914.4 6.1 psum.78
  920.5 81.2 %psum.79 = f32[16,16]{1,0:T(8,128)S(1)} all-reduce(f32[16,16]{1,0:T(8,128)S(1)} %psum.78), channel_id=1, replica_groups=mesh['gx_0'=2,'gx_1'=4,'gx_2'=2,'gy'=4,'gz'=16] {'gz'}, use_global_device_ids=true, to_apply=%region_52.53 | all-reduce | flops 256 | bytes 2048 | tf_op jit(solution)/shard_map/psum | solution.py:26
  (710 shorter events, 255.3 us)
Async XLA Ops:
  1.7 31.2 %collective-permute-start = (f32[16,1,4,128]{3,0,2,1:T(8,128)S(1)}, f32[16,1,4,128]{3,0,2,1:T(8,128)S(1)}, u32[]{:S(2)}, u32[]{:S(2)}) collective-permute-start(f32[16,1,4,128]{3,0,2,1:T(8,128)S(1)} %get-tuple-element.1257), channel_id=1, source_target_pairs={{0,64},{64,128},{128,192},{192,256},{256,320},{320,384},{384,448},... | collective-permute-start | bytes 98312 | tf_op jit(solution)/shard_map/ppermute | solution.py:18
  6.2 26.7 %collective-permute-start.1 = (f32[16,1,4,128]{3,0,2,1:T(8,128)S(1)}, f32[16,1,4,128]{3,0,2,1:T(8,128)S(1)}, u32[]{:S(2)}, u32[]{:S(2)}) collective-permute-start(f32[16,1,4,128]{3,0,2,1:T(8,128)S(1)} %get-tuple-element.1258), channel_id=1, source_target_pairs={{64,0},{128,64},{192,128},{256,192},{320,256},{384,320},{448,384},... | collective-permute-start | bytes 98312 | tf_op jit(solution)/shard_map/ppermute | solution.py:19
  34.3 7.1 collective-permute-start.3
  42.8 5.0 collective-permute-start.5
  49.0 5.1 collective-permute-start.6
  50.9 5.2 collective-permute-start.7
  58.1 6.2 collective-permute-start.9
  65.7 6.5 collective-permute-start.11
  72.6 7.3 collective-permute-start.12
  77.7 5.2 collective-permute-start.13
  85.9 5.7 collective-permute-start.15
  91.8 6.5 collective-permute-start.16
  96.6 5.8 collective-permute-start.17
  102.8 9.9 collective-permute-start.18
  110.7 20.2 %collective-permute-start.19 = (f32[16,1,4,128]{3,0,2,1:T(8,128)S(1)}, f32[16,1,4,128]{3,0,2,1:T(8,128)S(1)}, u32[]{:S(2)}, u32[]{:S(2)}) collective-permute-start(f32[16,1,4,128]{3,0,2,1:T(8,128)S(1)} %get-tuple-element.1252), channel_id=1, source_target_pairs={{64,0},{128,64},{192,128},{256,192},{320,256},{384,320},{448,384},... | collective-permute-start | bytes 98312 | tf_op jit(solution)/shard_map/ppermute | solution.py:19
  132.9 5.7 collective-permute-start.21
  138.7 5.3 collective-permute-start.22
  142.4 5.0 collective-permute-start.23
  147.8 24.2 %collective-permute-start.24 = (f32[16,1,4,128]{3,0,2,1:T(8,128)S(1)}, f32[16,1,4,128]{3,0,2,1:T(8,128)S(1)}, u32[]{:S(2)}, u32[]{:S(2)}) collective-permute-start(f32[16,1,4,128]{3,0,2,1:T(8,128)S(1)} %get-tuple-element.1249), channel_id=1, source_target_pairs={{0,64},{64,128},{128,192},{192,256},{256,320},{320,384},{384,448},... | collective-permute-start | bytes 98312 | tf_op jit(solution)/shard_map/ppermute | solution.py:18
  170.1 20.4 %collective-permute-start.25 = (f32[16,1,4,128]{3,0,2,1:T(8,128)S(1)}, f32[16,1,4,128]{3,0,2,1:T(8,128)S(1)}, u32[]{:S(2)}, u32[]{:S(2)}) collective-permute-start(f32[16,1,4,128]{3,0,2,1:T(8,128)S(1)} %get-tuple-element.1250), channel_id=1, source_target_pairs={{64,0},{128,64},{192,128},{256,192},{320,256},{384,320},{448,384},... | collective-permute-start | bytes 98312 | tf_op jit(solution)/shard_map/ppermute | solution.py:19
  192.5 5.7 collective-permute-start.27
  201.5 5.0 collective-permute-start.29
  206.9 11.4 %collective-permute-start.30 = (f32[16,1,4,128]{3,0,2,1:T(8,128)S(1)}, f32[16,1,4,128]{3,0,2,1:T(8,128)S(1)}, u32[]{:S(2)}, u32[]{:S(2)}) collective-permute-start(f32[16,1,4,128]{3,0,2,1:T(8,128)S(1)} %get-tuple-element.1247), channel_id=1, source_target_pairs={{0,64},{64,128},{128,192},{192,256},{256,320},{320,384},{384,448},... | collective-permute-start | bytes 98312 | tf_op jit(solution)/shard_map/ppermute | solution.py:18
  216.4 20.7 %collective-permute-start.31 = (f32[16,1,4,128]{3,0,2,1:T(8,128)S(1)}, f32[16,1,4,128]{3,0,2,1:T(8,128)S(1)}, u32[]{:S(2)}, u32[]{:S(2)}) collective-permute-start(f32[16,1,4,128]{3,0,2,1:T(8,128)S(1)} %get-tuple-element.1248), channel_id=1, source_target_pairs={{64,0},{128,64},{192,128},{256,192},{320,256},{384,320},{448,384},... | collective-permute-start | bytes 98312 | tf_op jit(solution)/shard_map/ppermute | solution.py:19
  239.1 5.7 collective-permute-start.33
  247.9 5.0 collective-permute-start.35
  253.3 11.3 %collective-permute-start.36 = (f32[16,1,4,128]{3,0,2,1:T(8,128)S(1)}, f32[16,1,4,128]{3,0,2,1:T(8,128)S(1)}, u32[]{:S(2)}, u32[]{:S(2)}) collective-permute-start(f32[16,1,4,128]{3,0,2,1:T(8,128)S(1)} %get-tuple-element.1245), channel_id=1, source_target_pairs={{0,64},{64,128},{128,192},{192,256},{256,320},{320,384},{384,448},... | collective-permute-start | bytes 98312 | tf_op jit(solution)/shard_map/ppermute | solution.py:18
  262.7 20.6 %collective-permute-start.37 = (f32[16,1,4,128]{3,0,2,1:T(8,128)S(1)}, f32[16,1,4,128]{3,0,2,1:T(8,128)S(1)}, u32[]{:S(2)}, u32[]{:S(2)}) collective-permute-start(f32[16,1,4,128]{3,0,2,1:T(8,128)S(1)} %get-tuple-element.1246), channel_id=1, source_target_pairs={{64,0},{128,64},{192,128},{256,192},{320,256},{384,320},{448,384},... | collective-permute-start | bytes 98312 | tf_op jit(solution)/shard_map/ppermute | solution.py:19
  285.3 5.7 collective-permute-start.39
  294.3 5.0 collective-permute-start.41
  299.7 11.2 %collective-permute-start.42 = (f32[16,1,4,128]{3,0,2,1:T(8,128)S(1)}, f32[16,1,4,128]{3,0,2,1:T(8,128)S(1)}, u32[]{:S(2)}, u32[]{:S(2)}) collective-permute-start(f32[16,1,4,128]{3,0,2,1:T(8,128)S(1)} %get-tuple-element.1243), channel_id=1, source_target_pairs={{0,64},{64,128},{128,192},{192,256},{256,320},{320,384},{384,448},... | collective-permute-start | bytes 98312 | tf_op jit(solution)/shard_map/ppermute | solution.py:18
  309.0 20.4 %collective-permute-start.43 = (f32[16,1,4,128]{3,0,2,1:T(8,128)S(1)}, f32[16,1,4,128]{3,0,2,1:T(8,128)S(1)}, u32[]{:S(2)}, u32[]{:S(2)}) collective-permute-start(f32[16,1,4,128]{3,0,2,1:T(8,128)S(1)} %get-tuple-element.1244), channel_id=1, source_target_pairs={{64,0},{128,64},{192,128},{256,192},{320,256},{384,320},{448,384},... | collective-permute-start | bytes 98312 | tf_op jit(solution)/shard_map/ppermute | solution.py:19
  331.7 5.7 collective-permute-start.45
  341.0 5.0 collective-permute-start.47
  346.3 11.4 %collective-permute-start.48 = (f32[16,1,4,128]{3,0,2,1:T(8,128)S(1)}, f32[16,1,4,128]{3,0,2,1:T(8,128)S(1)}, u32[]{:S(2)}, u32[]{:S(2)}) collective-permute-start(f32[16,1,4,128]{3,0,2,1:T(8,128)S(1)} %get-tuple-element.1241), channel_id=1, source_target_pairs={{0,64},{64,128},{128,192},{192,256},{256,320},{320,384},{384,448},... | collective-permute-start | bytes 98312 | tf_op jit(solution)/shard_map/ppermute | solution.py:18
  355.8 21.0 %collective-permute-start.49 = (f32[16,1,4,128]{3,0,2,1:T(8,128)S(1)}, f32[16,1,4,128]{3,0,2,1:T(8,128)S(1)}, u32[]{:S(2)}, u32[]{:S(2)}) collective-permute-start(f32[16,1,4,128]{3,0,2,1:T(8,128)S(1)} %get-tuple-element.1242), channel_id=1, source_target_pairs={{64,0},{128,64},{192,128},{256,192},{320,256},{384,320},{448,384},... | collective-permute-start | bytes 98312 | tf_op jit(solution)/shard_map/ppermute | solution.py:19
  378.9 5.7 collective-permute-start.51
  384.7 5.2 collective-permute-start.52
  387.8 5.0 collective-permute-start.53
  393.2 11.3 %collective-permute-start.54 = (f32[16,1,4,128]{3,0,2,1:T(8,128)S(1)}, f32[16,1,4,128]{3,0,2,1:T(8,128)S(1)}, u32[]{:S(2)}, u32[]{:S(2)}) collective-permute-start(f32[16,1,4,128]{3,0,2,1:T(8,128)S(1)} %get-tuple-element.1239), channel_id=1, source_target_pairs={{0,64},{64,128},{128,192},{192,256},{256,320},{320,384},{384,448},... | collective-permute-start | bytes 98312 | tf_op jit(solution)/shard_map/ppermute | solution.py:18
  402.4 20.5 %collective-permute-start.55 = (f32[16,1,4,128]{3,0,2,1:T(8,128)S(1)}, f32[16,1,4,128]{3,0,2,1:T(8,128)S(1)}, u32[]{:S(2)}, u32[]{:S(2)}) collective-permute-start(f32[16,1,4,128]{3,0,2,1:T(8,128)S(1)} %get-tuple-element.1240), channel_id=1, source_target_pairs={{64,0},{128,64},{192,128},{256,192},{320,256},{384,320},{448,384},... | collective-permute-start | bytes 98312 | tf_op jit(solution)/shard_map/ppermute | solution.py:19
  425.2 5.7 collective-permute-start.57
  434.2 5.0 collective-permute-start.59
  439.6 11.6 %collective-permute-start.60 = (f32[16,1,4,128]{3,0,2,1:T(8,128)S(1)}, f32[16,1,4,128]{3,0,2,1:T(8,128)S(1)}, u32[]{:S(2)}, u32[]{:S(2)}) collective-permute-start(f32[16,1,4,128]{3,0,2,1:T(8,128)S(1)} %get-tuple-element.1237), channel_id=1, source_target_pairs={{0,64},{64,128},{128,192},{192,256},{256,320},{320,384},{384,448},... | collective-permute-start | bytes 98312 | tf_op jit(solution)/shard_map/ppermute | solution.py:18
  449.1 21.0 %collective-permute-start.61 = (f32[16,1,4,128]{3,0,2,1:T(8,128)S(1)}, f32[16,1,4,128]{3,0,2,1:T(8,128)S(1)}, u32[]{:S(2)}, u32[]{:S(2)}) collective-permute-start(f32[16,1,4,128]{3,0,2,1:T(8,128)S(1)} %get-tuple-element.1238), channel_id=1, source_target_pairs={{64,0},{128,64},{192,128},{256,192},{320,256},{384,320},{448,384},... | collective-permute-start | bytes 98312 | tf_op jit(solution)/shard_map/ppermute | solution.py:19
  472.2 5.7 collective-permute-start.63
  480.9 5.0 collective-permute-start.65
  486.2 11.5 %collective-permute-start.66 = (f32[16,1,4,128]{3,0,2,1:T(8,128)S(1)}, f32[16,1,4,128]{3,0,2,1:T(8,128)S(1)}, u32[]{:S(2)}, u32[]{:S(2)}) collective-permute-start(f32[16,1,4,128]{3,0,2,1:T(8,128)S(1)} %get-tuple-element.1235), channel_id=1, source_target_pairs={{0,64},{64,128},{128,192},{192,256},{256,320},{320,384},{384,448},... | collective-permute-start | bytes 98312 | tf_op jit(solution)/shard_map/ppermute | solution.py:18
  495.7 20.9 %collective-permute-start.67 = (f32[16,1,4,128]{3,0,2,1:T(8,128)S(1)}, f32[16,1,4,128]{3,0,2,1:T(8,128)S(1)}, u32[]{:S(2)}, u32[]{:S(2)}) collective-permute-start(f32[16,1,4,128]{3,0,2,1:T(8,128)S(1)} %get-tuple-element.1236), channel_id=1, source_target_pairs={{64,0},{128,64},{192,128},{256,192},{320,256},{384,320},{448,384},... | collective-permute-start | bytes 98312 | tf_op jit(solution)/shard_map/ppermute | solution.py:19
  518.5 5.7 collective-permute-start.69
  527.2 5.0 collective-permute-start.71
  532.6 11.5 %collective-permute-start.72 = (f32[16,1,4,128]{3,0,2,1:T(8,128)S(1)}, f32[16,1,4,128]{3,0,2,1:T(8,128)S(1)}, u32[]{:S(2)}, u32[]{:S(2)}) collective-permute-start(f32[16,1,4,128]{3,0,2,1:T(8,128)S(1)} %get-tuple-element.1233), channel_id=1, source_target_pairs={{0,64},{64,128},{128,192},{192,256},{256,320},{320,384},{384,448},... | collective-permute-start | bytes 98312 | tf_op jit(solution)/shard_map/ppermute | solution.py:18
  542.1 20.8 %collective-permute-start.73 = (f32[16,1,4,128]{3,0,2,1:T(8,128)S(1)}, f32[16,1,4,128]{3,0,2,1:T(8,128)S(1)}, u32[]{:S(2)}, u32[]{:S(2)}) collective-permute-start(f32[16,1,4,128]{3,0,2,1:T(8,128)S(1)} %get-tuple-element.1234), channel_id=1, source_target_pairs={{64,0},{128,64},{192,128},{256,192},{320,256},{384,320},{448,384},... | collective-permute-start | bytes 98312 | tf_op jit(solution)/shard_map/ppermute | solution.py:19
  564.9 5.7 collective-permute-start.75
  573.5 5.0 collective-permute-start.77
  578.9 11.5 %collective-permute-start.78 = (f32[16,1,4,128]{3,0,2,1:T(8,128)S(1)}, f32[16,1,4,128]{3,0,2,1:T(8,128)S(1)}, u32[]{:S(2)}, u32[]{:S(2)}) collective-permute-start(f32[16,1,4,128]{3,0,2,1:T(8,128)S(1)} %get-tuple-element.1231), channel_id=1, source_target_pairs={{0,64},{64,128},{128,192},{192,256},{256,320},{320,384},{384,448},... | collective-permute-start | bytes 98312 | tf_op jit(solution)/shard_map/ppermute | solution.py:18
  588.4 20.8 %collective-permute-start.79 = (f32[16,1,4,128]{3,0,2,1:T(8,128)S(1)}, f32[16,1,4,128]{3,0,2,1:T(8,128)S(1)}, u32[]{:S(2)}, u32[]{:S(2)}) collective-permute-start(f32[16,1,4,128]{3,0,2,1:T(8,128)S(1)} %get-tuple-element.1232), channel_id=1, source_target_pairs={{64,0},{128,64},{192,128},{256,192},{320,256},{384,320},{448,384},... | collective-permute-start | bytes 98312 | tf_op jit(solution)/shard_map/ppermute | solution.py:19
  611.2 5.7 collective-permute-start.81
  617.0 6.0 collective-permute-start.82
  619.8 5.0 collective-permute-start.83
  625.4 223.7 %collective-permute-start.84 = (f32[16,1,4,128]{3,0,2,1:T(8,128)S(1)}, f32[16,1,4,128]{3,0,2,1:T(8,128)S(1)}, u32[]{:S(2)}, u32[]{:S(2)}) collective-permute-start(f32[16,1,4,128]{3,0,2,1:T(8,128)S(1)} %get-tuple-element.1229), channel_id=1, source_target_pairs={{0,64},{64,128},{128,192},{192,256},{256,320},{320,384},{384,448},... | collective-permute-start | bytes 98312 | tf_op jit(solution)/shard_map/ppermute | solution.py:18
  634.9 214.3 %collective-permute-start.85 = (f32[16,1,4,128]{3,0,2,1:T(8,128)S(1)}, f32[16,1,4,128]{3,0,2,1:T(8,128)S(1)}, u32[]{:S(2)}, u32[]{:S(2)}) collective-permute-start(f32[16,1,4,128]{3,0,2,1:T(8,128)S(1)} %get-tuple-element.1230), channel_id=1, source_target_pairs={{64,0},{128,64},{192,128},{256,192},{320,256},{384,320},{448,384},... | collective-permute-start | bytes 98312 | tf_op jit(solution)/shard_map/ppermute | solution.py:19
  849.3 5.1 collective-permute-start.86
  852.4 5.7 collective-permute-start.87
  (31 other events, 987.9 us)
where the time goes:
time: 1060 us; the launch traced here: 1050 us
  waiting for transfers between devices  328 us (31%)
  blocking collectives  324 us (31%)
  starting transfers between devices  289 us (27%)
  other arithmetic  62.8 us (6%)
  local copies, waits for them, and re-layouts  32.7 us (3%)
  between operations  11.4 us (1%)
    psum x10, blocking collectives, one_axis_at_a_time(): value = lax.psum(value, axis)  324 us
    ppermute x45, waiting for transfers between devices, with_halo(): after = lax.ppermute(first, axis, down)  319 us
    ppermute x45, starting transfers between devices, with_halo(): before = lax.ppermute(last, axis, up)  209 us
    ppermute x45, starting transfers between devices, with_halo(): after = lax.ppermute(first, axis, down)  79.6 us
  transfers between devices with their start and end apart: 90, of which 59 were waited for; matrix products, arithmetic and copies ran while one was open for 4% of the time, Pallas kernels for 0%

commit v1 on v0

v1 whole, which is shorter than its diff:
```python
import functools

import jax
import jax.numpy as jnp
from jax import lax
from jax.experimental import pallas as pl
from jax.experimental.pallas import tpu as pltpu
from jax.sharding import PartitionSpec as P

RHS = 16
LX = 2
LZ = 4
LY = 128
LINES = LX * LZ
WIDE = 2 * LY
LO0, HI0 = 2, 1
LO1, HI1 = 4, 3
N0 = LO0 + LZ + HI0
N1 = LO1 + LZ + HI1
CORES = 2
HIGHEST = lax.Precision.HIGHEST
MESH = pl.DeviceIdType.MESH
AXES = ("gx", "gy", "gz")


class Place:
    def __init__(self, sizes, xs):
        self.gx, self.gy, self.gz = sizes
        self.xs = xs
        self.zs = self.gx // (CORES * xs) * self.gz
        self.g, self.m, self.h = (lax.axis_index(a) for a in AXES)
        self.core = lax.rem(self.g, CORES)
        self.x = lax.rem(self.g // CORES, xs)
        self.z = self.g // (CORES * xs) * self.gz + self.h

    def chip(self, dx, dy, dz, other_core=False):
        x = lax.rem(self.x + dx + self.xs, self.xs)
        y = lax.rem(self.m + dy + self.gy, self.gy)
        z = lax.rem(self.z + dz + self.zs, self.zs)
        core = 1 - self.core if other_core else self.core
        return (z // self.gz * (CORES * self.xs) + x * CORES + core, y, lax.rem(z, self.gz))


def plane_offsets(place):
    return [(dx, dy) for dx in range(place.xs) for dy in range(place.gy) if (dx, dy) != (0, 0)]


def window_of(zs):
    return 4 if zs > 4 else 2


def window_offsets(zs):
    return (-1, 1, 2) if window_of(zs) == 4 else (1,)


def stride_offsets(zs):
    return list(range(window_of(zs), zs, window_of(zs)))


def sides(value):
    return pltpu.roll(value, 1, 1) + pltpu.roll(value, WIDE - 1, 1)


def ybox(value):
    return value + sides(value)


def line_of(ref, line):
    return ref[pl.ds(line, RHS, stride=LINES), :]


def invert(matrix, target, order):
    rows = lax.broadcasted_iota(jnp.int32, (order, 128), 0)
    columns = [jnp.broadcast_to(matrix[:, j : j + 1], (order, 128)) for j in range(order)]
    for k in range(order):
        pivot = 1.0 / jnp.broadcast_to(columns[k][k : k + 1, :], (order, 128))
        own = rows == k
        for j in range(k + 1, order):
            scaled = jnp.broadcast_to(columns[j][k : k + 1, :], (order, 128)) * pivot
            columns[j] = jnp.where(own, scaled, columns[j] - columns[k] * scaled)
        scaled = jnp.broadcast_to(target[k : k + 1, :], (order, 128)) * pivot
        target = jnp.where(own, scaled, target - columns[k] * scaled)
    return target


def exchange_kernel(
    sizes, xs,
    res_ref, dirp_ref, imgp_ref, gram_ref,
    smooth_ref, image_ref, total_ref, inverse_ref,
    r0, r1, up, down, upin, downin, f_ref, s1, s0, masks, y_ref, send3, u3, u3in,
    ar_send, ar_in,
    send0, recv0, send1, recv1, send2, recv2, send3s, recv3s, send_ar, recv_ar,
):
    place = Place(sizes, xs)
    g, m, h = place.g, place.m, place.h
    zero = jnp.zeros((RHS, LY), jnp.float32)
    below_z, above_z = h > 0, h < place.gz - 1
    below_y, above_y = m > 0, m < place.gy - 1
    below_x, above_x = g > 0, g < place.gx - 1

    @pl.when(jnp.logical_not(below_z & above_z & below_y & above_y & below_x & above_x))
    def _():
        for i in range(N0):
            for s in range(3):
                r0[s, i] = zero
        for p in range(2):
            for i in range(N1):
                for s in range(3):
                    r1[p, s, i] = zero
        for j in range(LZ):
            upin[j] = zero
            downin[j] = zero
            u3in[j] = zero
        s0[LZ + 1] = jnp.zeros((RHS, WIDE), jnp.float32)

    barrier = pltpu.get_barrier_semaphore()
    near = []
    for dz in (-1, 0, 1):
        for dy in (-1, 0, 1):
            if (dz, dy) != (0, 0):
                cond = True
                cond = cond & (below_z if dz < 0 else above_z) if dz else cond
                cond = cond & (below_y if dy < 0 else above_y) if dy else cond
                near.append((cond, (g, m + dy, h + dz)))
    near.append((below_x, (g - 1, m, h)))
    near.append((above_x, (g + 1, m, h)))
    always = [place.chip(0, 0, 0, True)]
    always += [place.chip(dx, dy, 0) for dx, dy in plane_offsets(place)]
    offs = set(window_offsets(place.zs)) | {-o for o in window_offsets(place.zs)} | set(stride_offsets(place.zs))
    always += [place.chip(0, 0, dz) for dz in sorted({o % place.zs for o in offs})]
    expected = len(always)
    for cond, device in near:
        expected = expected + jnp.where(cond, 1, 0)

        @pl.when(cond)
        def _(device=device):
            pl.semaphore_signal(barrier, inc=1, device_id=device, device_id_type=MESH)

    for device in always:
        pl.semaphore_signal(barrier, inc=1, device_id=device, device_id_type=MESH)

    lane = lax.broadcasted_iota(jnp.int32, (RHS, WIDE), 1)
    inside = (lane < LY) | ((lane < LY + LY // 2) & above_y) | ((lane >= LY + LY // 2) & below_y)
    scale = jnp.where(inside, jnp.float32(1 / 26), jnp.float32(0))
    even = jnp.where(lax.rem(lane, 2) == 0, scale, jnp.float32(0))
    odd = scale - even
    for t, keep in enumerate((True, below_z, above_z)):
        weight = jnp.float32(1) if t == 0 else jnp.where(keep, jnp.float32(1), jnp.float32(0))
        masks[t, 0] = even * weight
        masks[t, 1] = odd * weight
    for j in range(LZ):
        r0[0, LO0 + j] = line_of(res_ref, j)
    ident = jnp.where(
        lax.broadcasted_iota(jnp.int32, (RHS, 128), 0) == lax.broadcasted_iota(jnp.int32, (RHS, 128), 1),
        jnp.float32(1), jnp.float32(0),
    )
    gram = gram_ref[...]
    sym = 0.5 * (gram + gram.T)
    inverse_ref[...] = invert(sym, ident, RHS)
    gram_pq = jnp.zeros((RHS, 128), jnp.float32)
    for line in range(LINES):
        right = jnp.concatenate([zero[:8]] * 6 + [line_of(imgp_ref, line)] + [zero[:8]] * 8, axis=0)
        gram_pq += lax.dot_general(
            line_of(dirp_ref, line), right, (((1,), (1,)), ((), ())), precision=HIGHEST, preferred_element_type=jnp.float32
        )

    pl.semaphore_wait(barrier, expected)

    def mask(j, parity):
        return masks[0 if 0 <= j < LZ else 1 if j < 0 else 2, parity]

    def start(copies):
        for cond, copy in copies:
            pl.when(cond)(copy.start)

    def finish(copies):
        for cond, copy in copies:
            pl.when(cond)(copy.wait_send)

    def around(buf, low, high, before, send_sems, recv_sems):
        out = []
        cond_z = {-1: below_z, 1: above_z}
        cond_y = {-1: below_y, 1: above_y}
        n = 0
        for dz in (0, 1, -1):
            for dy in (0, 1, -1):
                if (dz, dy) == (0, 0):
                    continue
                src, size = (low, LZ) if dz == 0 else (low + LZ - before, before) if dz > 0 else (low, high)
                dst = low if dz == 0 else 0 if dz > 0 else low + LZ
                slot = 0 if dy == 0 else 1 if dy > 0 else 2
                copy = pltpu.make_async_remote_copy(
                    src_ref=buf.at[0, pl.ds(src, size)],
                    dst_ref=buf.at[slot, pl.ds(dst, size)],
                    send_sem=send_sems.at[n], recv_sem=recv_sems.at[n],
                    device_id=(g, m + dy, h + dz), device_id_type=MESH,
                )
                to, came = True, True
                if dz:
                    to, came = to & cond_z[dz], came & cond_z[-dz]
                if dy:
                    to, came = to & cond_y[dy], came & cond_y[-dy]
                out.append((to, came, copy))
                n += 1
        return out

    def wide(buf, i):
        lane_half = lax.broadcasted_iota(jnp.int32, (RHS, LY), 1) < LY // 2
        return jnp.concatenate([buf[0, i], jnp.where(lane_half, buf[2, i], buf[1, i])], axis=1)

    copies0 = around(r0, LO0, HI0, LO0, send0, recv0)
    start([(to, copy) for to, _, copy in copies0])
    for _, came, copy in copies0:
        pl.when(came)(copy.wait_recv)

    rw = {j: wide(r0, LO0 + j) for j in range(-LO0, LZ + HI0)}
    fe = {}
    for j in range(-LO0, LZ + HI0, 2):
        e = rw[j] * mask(j, 0)
        o = (rw[j] + sides(e)) * mask(j, 1)
        fe[j] = e
        f_ref[LO0 + j] = e + o
    for j in range(-1, LZ, 2):
        n = rw[j] + ybox(f_ref[LO0 + j - 1] + f_ref[LO0 + j + 1])
        e = n * mask(j, 0)
        o = (n + sides(e)) * mask(j, 1)
        fe[j] = e
        f_ref[LO0 + j] = e + o

    for j in range(LZ):
        box = ybox(f_ref[LO0 + j - 1] + f_ref[LO0 + j] + f_ref[LO0 + j + 1])[:, :LY]
        down[j] = box
        up[j] = line_of(res_ref, LZ + j) + box
    to_up = pltpu.make_async_remote_copy(
        src_ref=up, dst_ref=upin, send_sem=send1.at[0], recv_sem=recv1.at[0], device_id=(g + 1, m, h), device_id_type=MESH
    )
    to_down = pltpu.make_async_remote_copy(
        src_ref=down, dst_ref=downin, send_sem=send1.at[1], recv_sem=recv1.at[1], device_id=(g - 1, m, h), device_id_type=MESH
    )
    start([(above_x, to_up), (below_x, to_down)])

    pl.when(below_x)(to_up.wait_recv)
    keep = jnp.where(below_x, jnp.float32(1), jnp.float32(0))
    for j in range(LZ):
        r1[0, 0, LO1 + j] = (upin[j] + down[j]) * keep
    low = around(r1.at[0], LO1, HI1, LO1, send2.at[0], recv2.at[0])
    start([(to, copy) for to, _, copy in low])
    pl.when(above_x)(to_down.wait_recv)
    for j in range(LZ):
        r1[1, 0, LO1 + j] = downin[j] + up[j]
    high = around(r1.at[1], LO1, HI1, LO1, send2.at[1], recv2.at[1])
    start([(to, copy) for to, _, copy in high])
    for _, came, copy in low + high:
        pl.when(came)(copy.wait_recv)

    for p in range(2):
        r = {j: wide(r1.at[p], LO1 + j) for j in range(-LO1, LZ + HI1)}
        evens = {}
        for j in range(-LO1, LZ + HI1, 2):
            e = r[j] * mask(j, 0)
            o = (r[j] + sides(e)) * mask(j, 1)
            evens[j] = e
            s1[p, LO1 + j] = e + o
        for j in range(1 - LO1, LZ + HI1 - 1, 2):
            n = r[j] + ybox(s1[p, LO1 + j - 1] + s1[p, LO1 + j + 1])
            e = n * mask(j, 0)
            o = (n + sides(e)) * mask(j, 1)
            e = (n + sides(o)) * mask(j, 0)
            s1[p, LO1 + j] = e + o
        for j in range(2 - LO1, LZ + HI1 - 2, 2):
            n = r[j] + ybox(s1[p, LO1 + j - 1] + s1[p, LO1 + j + 1])
            o = (n + sides(evens[j])) * mask(j, 1)
            e = (n + sides(o)) * mask(j, 0)
            s1[p, LO1 + j] = e + o

    def odd_sum(j):
        both = [s1[0, LO1 + i] + s1[1, LO1 + i] for i in (j - 1, j, j + 1)]
        return ybox(both[0] + both[1] + both[2])

    for j in range(-1, LZ):
        y_ref[1 + j] = odd_sum(j)
    for j in range(-1, LZ, 2):
        n = rw[j] + y_ref[1 + j] + ybox(f_ref[LO0 + j - 1] + f_ref[LO0 + j + 1])
        o = (n + sides(fe[j])) * mask(j, 1)
        e = (n + sides(o)) * mask(j, 0)
        s0[1 + j] = e + o
    for j in range(0, LZ, 2):
        n = rw[j] + y_ref[1 + j] + ybox(s0[1 + j - 1] + s0[1 + j + 1])
        o = (n + sides(fe[j])) * mask(j, 1)
        e = (n + sides(o)) * mask(j, 0)
        s0[1 + j] = e + o

    send3[...] = s0[1]
    to_z = pltpu.make_async_remote_copy(
        src_ref=send3, dst_ref=s0.at[LZ + 1], send_sem=send3s.at[0], recv_sem=recv3s.at[0],
        device_id=(g, m, h - 1), device_id_type=MESH,
    )
    start([(below_z, to_z)])

    sums = gram_pq
    for a in range(LX):
        for j in range(LZ):
            line = a * LZ + j
            own = s0[1 + j] if a == 0 else s1[1, LO1 + j]
            if a == 0:
                half = y_ref[1 + j] + ybox(s0[j]) + pltpu.roll(own, 1, 1)
            else:
                half = ybox(s1[1, LO1 + j - 1]) + pltpu.roll(own, 1, 1)
            half = (13.0 * own - half)[:, :LY]
            own = own[:, :LY]
            smooth_ref[line] = own
            right = jnp.concatenate([line_of(res_ref, line), line_of(imgp_ref, line), half] + [zero[:8]] * 10, axis=0)
            sums += lax.dot_general(
                own, right, (((1,), (1,)), ((), ())), precision=HIGHEST, preferred_element_type=jnp.float32
            )
    value = sums[:8] + pltpu.roll(sums[8:], 64, 1)

    def to_all(devices, value, slot):
        ar_send[slot] = value
        copies = []
        for i, device in enumerate(devices):
            copies.append(
                pltpu.make_async_remote_copy(
                    src_ref=ar_send.at[slot], dst_ref=ar_in.at[first[slot] + i],
                    send_sem=send_ar.at[first[slot] + i], recv_sem=recv_ar.at[first[slot] + i],
                    device_id=device, device_id_type=MESH,
                )
            )
        for copy in copies:
            copy.start()
        return copies

    def collect(copies, value, slot):
        for i, copy in enumerate(copies):
            copy.wait_recv()
            value = value + ar_in[first[slot] + i]
        return value

    groups = [
        [place.chip(0, 0, 0, True)],
        [place.chip(dx, dy, 0) for dx, dy in plane_offsets(place)],
        [place.chip(0, 0, -dz) for dz in window_offsets(place.zs)],
        [place.chip(0, 0, dz) for dz in stride_offsets(place.zs)],
    ]
    first = [sum(len(q) for q in groups[:i]) for i in range(len(groups))]
    sent = []
    for slot in range(3):
        copies = to_all(groups[slot], value, slot)
        sent += copies
        value = collect(copies, value, slot)
        if slot == 0:
            pl.when(above_z)(to_z.wait_recv)
            for j in range(LZ):
                u3[j] = ybox(s0[j] + s0[1 + j] + s0[2 + j])[:, :LY]
            to_x = pltpu.make_async_remote_copy(
                src_ref=u3, dst_ref=u3in, send_sem=send3s.at[1], recv_sem=recv3s.at[1],
                device_id=(g - 1, m, h), device_id_type=MESH,
            )
            start([(below_x, to_x)])
    copies = to_all(groups[3], value, 3)
    sent += copies
    for j in range(LZ):
        image_ref[j] = 27.0 * s0[1 + j][:, :LY] - (y_ref[1 + j][:, :LY] + u3[j])
    pl.when(above_x)(to_x.wait_recv)
    for j in range(LZ):
        box = ybox(s1[1, LO1 + j - 1] + s1[1, LO1 + j] + s1[1, LO1 + j + 1])[:, :LY]
        image_ref[LZ + j] = 27.0 * s1[1, LO1 + j][:, :LY] - (box + u3[j] + u3in[j])
    value = collect(copies, value, 3)
    total_ref[...] = value

    finish([(to, copy) for to, _, copy in copies0 + low + high])
    finish([(above_x, to_up), (below_x, to_down), (below_z, to_z), (below_x, to_x)])
    for copy in sent:
        copy.wait_send()


def update_kernel(
    sol_ref, res_ref, dirp_ref, imgp_ref, smooth_ref, image_ref, total_ref, inverse_ref, sol_out, res_out, dir_out
):
    def dot(a, b, ca=1, cb=0):
        return lax.dot_general(a, b, (((ca,), (cb,)), ((), ())), precision=HIGHEST, preferred_element_type=jnp.float32)

    total = total_ref[...]
    both = jnp.concatenate([total, pltpu.roll(total, 64, 1)], axis=0)
    gram, cross, half, prev = (both[:, RHS * i : RHS * (i + 1)] for i in range(4))
    beta = dot(inverse_ref[...][:, :RHS], gram)
    mixed = dot(cross, beta)
    curved = half + mixed
    curvature = curved + curved.T + dot(beta, dot(0.5 * (prev + prev.T), beta), 0, 0)
    curvature = 0.5 * (curvature + curvature.T)
    alpha = invert(curvature, jnp.concatenate([gram] * 8, axis=1), RHS)[:, :RHS]

    def all_lines(ref):
        return jnp.concatenate([line_of(ref, line) for line in range(LINES)], axis=1)

    smooth = jnp.concatenate([smooth_ref[line] for line in range(LINES)], axis=1)
    image = jnp.concatenate([image_ref[line] for line in range(LINES)], axis=1)
    direction = smooth + dot(beta, all_lines(dirp_ref), 0, 0)
    image_new = image + dot(beta, all_lines(imgp_ref), 0, 0)
    sol_new = all_lines(sol_ref) + dot(alpha, direction, 0, 0)
    res_new = all_lines(res_ref) - dot(alpha, image_new, 0, 0)
    for line in range(LINES):
        at = slice(line * LY, (line + 1) * LY)
        dir_out[pl.ds(line, RHS, stride=LINES), :] = direction[:, at]
        sol_out[pl.ds(line, RHS, stride=LINES), :] = sol_new[:, at]
        res_out[pl.ds(line, RHS, stride=LINES), :] = res_new[:, at]


def build(mesh, xs):
    sizes = tuple(mesh.shape[a] for a in AXES)
    zs = sizes[0] // (CORES * xs) * sizes[2]
    slots = 1 + (xs * sizes[1] - 1) + len(window_offsets(zs)) + len(stride_offsets(zs))
    f32 = jnp.float32
    vmem = pl.BlockSpec(memory_space=pltpu.VMEM)

    def body(solution, residual, direction_prev, image_prev, gram_prev):
        flat = (RHS * LINES, LY)
        sol, res, dirp, imgp = (a.reshape(flat) for a in (solution, residual, direction_prev, image_prev))
        field = jax.ShapeDtypeStruct((LINES, RHS, LY), f32)
        dma = pltpu.SemaphoreType.DMA
        smooth, image, total, inverse = pl.pallas_call(
            functools.partial(exchange_kernel, sizes, xs),
            name="exchange",
            out_shape=(field, field, jax.ShapeDtypeStruct((8, 128), f32), jax.ShapeDtypeStruct((RHS, 128), f32)),
            in_specs=[vmem] * 4,
            out_specs=(vmem,) * 4,
            scratch_shapes=[
                pltpu.VMEM((3, N0, RHS, LY), f32),
                pltpu.VMEM((2, 3, N1, RHS, LY), f32),
                *[pltpu.VMEM((LZ, RHS, LY), f32)] * 4,
                pltpu.VMEM((N0, RHS, WIDE), f32),
                pltpu.VMEM((2, N1, RHS, WIDE), f32),
                pltpu.VMEM((LZ + 2, RHS, WIDE), f32),
                pltpu.VMEM((3, 2, RHS, WIDE), f32),
                pltpu.VMEM((LZ + 1, RHS, WIDE), f32),
                pltpu.VMEM((RHS, WIDE), f32),
                *[pltpu.VMEM((LZ, RHS, LY), f32)] * 2,
                pltpu.VMEM((4, 8, 128), f32),
                pltpu.VMEM((slots, 8, 128), f32),
                dma((8,)), dma((8,)), dma((2,)), dma((2,)), dma((2, 8)), dma((2, 8)), dma((2,)), dma((2,)),
                dma((slots,)), dma((slots,)),
            ],
            compiler_params=pltpu.CompilerParams(collective_id=0, has_side_effects=True),
        )(res, dirp, imgp, gram_prev)
        out = jax.ShapeDtypeStruct(flat, f32)
        sol_new, res_new, direction = pl.pallas_call(
            update_kernel,
            name="update",
            out_shape=(out, out, out),
            in_specs=[vmem] * 8,
            out_specs=(vmem,) * 3,
        )(sol, res, dirp, imgp, smooth, image, total, inverse)
        return tuple(a.reshape(solution.shape) for a in (sol_new, res_new, direction))

    field = P(None, "gx", "gz", "gy")
    return jax.shard_map(
        body, mesh=mesh, in_specs=(field,) * 4 + (P(),), out_specs=(field,) * 3, check_vma=False
    )


def solution(mesh):
    return build(mesh, xs=4)
```

time: 1060 us -> 81.1 us (0.08)
  the two profiles are of different devices: /device:TPU:1 before, /device:TPU:4 now
where the time goes in v1:
time: 81.1 us; the launch traced here: 80.8 us
  Pallas kernels  80.2 us (99%)
    pallas_call x1, Pallas kernels, body(): pl.pallas_call(functools.partial(exchange_kernel, sizes, xs), name='excha...  76.8 us
    pallas_call x1, Pallas kernels, body(): pl.pallas_call(update_kernel, name='update', out_shape=(out, out, out), i...  3.42 us

profile of v1, /device:TPU:4, one launch (start us, length us, event | category | flops | bytes accessed | tf_op | source)
XLA Modules:
  0.0 80.8 jit_solution(13436994376540023177)
XLA Ops:
  0.6 76.8 %exchange.1 = (f32[8,16,128]{2,1,0:T(8,128)}, f32[8,16,128]{2,1,0:T(8,128)}, f32[8,128]{1,0:T(8,128)}, f32[16,128]{1,0:T(8,128)}) custom-call(f32[128,128]{1,0:T(8,128)} %bitcast.7, f32[128,128]{1,0:T(8,128)} %bitcast.9, f32[128,128]{1,0:T(8,128)} %bitcast.11, f32[16,16]{1,0:T(8,128)} %gram_ref.1), custom_call_target="tpu_custom_call" | custom-call | tf_op jit(solution)/shard_map/exchange/pallas_call | solution.py:421
  77.4 3.4 %update.1 = (f32[128,128]{1,0:T(8,128)}, f32[128,128]{1,0:T(8,128)}, f32[128,128]{1,0:T(8,128)}) custom-call(f32[128,128]{1,0:T(8,128)} %bitcast.13, f32[128,128]{1,0:T(8,128)} %bitcast.8, f32[128,128]{1,0:T(8,128)} %bitcast.10, f32[128,128]{1,0:T(8,128)} %bitcast.12, f32[8,16,128]{2,1,0:T(8,128)} %get-tuple-element.10.smooth_ref, ...), custom_call_target="tpu_custom_call" | custom-call | tf_op jit(solution)/shard_map/update/pallas_call | solution.py:446
